TPU v7x, 256 devices: a whole 4x4x8 slice. The times are simulated.
256 devices in a mesh: gx: 8 (over z), gy: 32 (over x, y, core).
Axes of the slice: x: 4, y: 4, z: 8, core: 2. Of those that a mesh axis runs over, the one named last changes fastest.
Arguments:
- right_side: float32 [4096, 16384], P('gx', 'gy'), may hold values from -8 to 8
- drift_x: float32 [4096, 16384], P('gx', 'gy'), may hold values from -0.9 to 0.9
- drift_y: float32 [4096, 16384], P('gx', 'gy'), may hold values from -0.9 to 0.9
- sketch_rows: float32 [256, 4096], P(None, 'gx'), may hold values from -0.375 to 0.375
- sketch_cols: float32 [256, 16384], P(None, 'gy'), may hold values from -6 to 6
Outputs:
- solution: float32 [4096, 16384], P('gx', 'gy')
- residual: float32 [4096, 16384], P('gx', 'gy')
All inputs are finite; a program needn't handle non-finite values.
Results may differ from a plain program's by a relative error of at most 0.0003.
Values sent between devices are 32-bit elements; how exact they have to be, the bound alone decides.
No kernel may reach another device: no remote copies, remote signals or barrier semaphores. Data moves between devices by JAX's collectives and lax.ppermute only.
A program may use at most 64 MiB of HBM per device.

v0:
```python
import jax
import jax.numpy as jnp
from jax import lax
from jax.sharding import Mesh
from jax.sharding import PartitionSpec as P

ITERS = 4
GY = ("gy_0", "gy_1", "gy_2")


shift_value = 0.05


def sent_to_all(value, axis):
    copies = jnp.broadcast_to(value, (lax.axis_size(axis), *value.shape))
    return lax.all_to_all(copies, axis, split_axis=0, concat_axis=0, tiled=True)


def of_everyone(value, axis):
    everything = sent_to_all(value, axis)
    return jnp.sum(everything, axis=0)


def one_axis_at_a_time(value, axes):
    far, near = axes
    return of_everyone(of_everyone(value, near), far)


def with_halo(value, sides, width):
    edges = {}
    for axis, dim in sides:
        size, length = (lax.axis_size(axis), value.shape[dim])
        up = [(i, (i + 1) % size) for i in range(size - 1)]
        last = lax.slice_in_dim(value, length - width, length, axis=dim)
        initial = lax.slice_in_dim(value, 0, width, axis=dim)
        edges[dim] = (
            lax.ppermute(last, axis, up),
            lax.ppermute(initial, axis, [(b, a) for a, b in up]),
        )
    done = []
    for _, dim in sides:
        low, high = edges[dim]
        around = [(width, width) if d in done else (0, 0) for d in range(value.ndim)]
        value = jnp.concatenate([jnp.pad(low, around), value, jnp.pad(high, around)], axis=dim)
        done.append(dim)
    return value


def stencil(padded, field, drift_x, drift_y):
    upper_cells = padded[:-2, 1:-1]
    lower_cells = padded[2:, 1:-1]
    left_cells = padded[1:-1, :-2]
    right_cells = padded[1:-1, 2:]
    return (
        (4.0 + shift_value) * field
        - (1.0 + drift_x) * upper_cells
        - (1.0 - drift_x) * lower_cells
        - (1.0 + drift_y) * left_cells
        - (1.0 - drift_y) * right_cells
    )


def solve_small(hessenberg, beta_norm):
    gram_matrix = jnp.dot(hessenberg.T, hessenberg, precision=lax.Precision.HIGHEST)
    target = beta_norm * hessenberg[0]
    factor = jnp.linalg.cholesky(gram_matrix)
    count = hessenberg.shape[1]
    forward = []
    for row in range(count):
        acc = target[row]
        for col in range(row):
            acc = acc - factor[row, col] * forward[col]
        forward.append(acc / factor[row, row])
    backward = [None] * count
    for row in reversed(range(count)):
        acc = forward[row]
        for col in range(row + 1, count):
            acc = acc - factor[col, row] * backward[col]
        backward[row] = acc / factor[row, row]
    return backward


def body(right_side, drift_x, drift_y, sketch_rows, sketch_cols):

    def sketch(field):
        product = jnp.dot(field, sketch_cols.T, precision=lax.Precision.HIGHEST)
        partial_value = jnp.einsum(
            "ki,ik->k", sketch_rows, product, precision=lax.Precision.HIGHEST
        )
        return one_axis_at_a_time(partial_value, (("gx", "gy_0"), ("gy_1", "gy_2")))

    first_sketch = sketch(right_side)
    beta_norm = jnp.sqrt(jnp.sum(first_sketch * first_sketch))
    basis_vectors = [right_side / beta_norm]
    sketched = [first_sketch / beta_norm]
    images = []
    columns = []
    for column in range(ITERS):
        current = basis_vectors[column]
        padded = with_halo(current, (("gx", 0), (GY, 1)), 1)
        applied = stencil(padded, current, drift_x, drift_y)
        images.append(applied)
        sketch_image = sketch(applied)
        sketch_matrix = jnp.stack(sketched, axis=1)
        projection = jnp.dot(sketch_matrix.T, sketch_image, precision=lax.Precision.HIGHEST)
        remainder = applied
        for index_prev in range(column + 1):
            remainder = remainder - projection[index_prev] * basis_vectors[index_prev]
        remainder_sketch = sketch_image - jnp.dot(
            sketch_matrix, projection, precision=lax.Precision.HIGHEST
        )
        new_norm = jnp.sqrt(jnp.sum(remainder_sketch * remainder_sketch))
        basis_vectors.append(remainder / new_norm)
        sketched.append(remainder_sketch / new_norm)
        entries = jnp.concatenate(
            [projection, new_norm[None], jnp.zeros((ITERS - column - 1,), jnp.float32)]
        )
        columns.append(entries)
    hessenberg = jnp.stack(columns, axis=1)
    coeffs = solve_small(hessenberg, beta_norm)
    solution = jnp.zeros_like(right_side)
    for column in range(ITERS):
        solution = solution + coeffs[column] * basis_vectors[column]
    residual = right_side
    for column in range(ITERS):
        residual = residual - coeffs[column] * images[column]
    return (solution, residual)


def solution(mesh):
    split = Mesh(mesh.devices.reshape(mesh.shape["gx"], 4, 4, 2), ("gx", "gy_0", "gy_1", "gy_2"))
    in_specs = (P("gx", GY), P("gx", GY), P("gx", GY), P(None, "gx"), P(None, GY))
    out_specs = (P("gx", GY), P("gx", GY))
    return jax.shard_map(body, mesh=split, in_specs=in_specs, out_specs=out_specs, check_vma=False)
```

profile of v0, /device:TPU:1, one launch (start us, length us, event | category | flops | bytes accessed | tf_op | source)
XLA Modules:
  0.0 276.0 jit_solution(3858249850533486412)
XLA Ops:
  1.7 2.3 convolution_bitcast_fusion.4
  4.4 10.4 %all_to_all.60 = f32[8,1,256]{2,1,0:T(1,128)S(1)} all-to-all(f32[8,1,256]{2,1,0:T(1,128)S(1)} %broadcast_in_dim.42), channel_id=1, replica_groups=mesh['gx'=8,'gy_0'=4,'gy_1'=4,'gy_2'=2] {'gy_1','gy_2'}, dimensions={0} | all-to-all | bytes 16384 | tf_op jit(solution)/shard_map/all_to_all | solution.py:16
  14.8 19.5 %all_to_all.61 = f32[32,1,256]{2,1,0:T(1,128)S(1)} all-to-all(f32[32,1,256]{2,1,0:T(1,128)S(1)} %broadcast_in_dim.43), channel_id=1, replica_groups=mesh['gx'=8,'gy_0'=4,'gy_1'=4,'gy_2'=2] {'gx','gy_0'}, dimensions={0} | all-to-all | bytes 65536 | tf_op jit(solution)/shard_map/all_to_all | solution.py:16
  36.0 2.4 collective-permute-start
  38.4 1.3 collective-permute-start.1
  39.7 4.5 %collective-permute-start.2 = (f32[512,1]{1,0:T(8,128)S(1)}, f32[512,1]{1,0:T(8,128)S(1)}, u32[]{:S(2)}, u32[]{:S(2)}) collective-permute-start(f32[512,1]{1,0:T(8,128)S(1)} %get-tuple-element.20), channel_id=1, source_target_pairs={{0,1},{1,2},{2,3},{3,4},{4,5},{5,6},{6,7},{7,8},{8,9},{9,10},{10,1... | collective-permute-start | bytes 6152 | tf_op jit(solution)/shard_map/ppermute | solution.py:37
  44.2 1.9 collective-permute-start.3
  46.1 1.3 collective-permute-done.2
  47.5 4.4 %collective-permute-done.3 = f32[512,1]{1,0:T(8,128)S(1)} collective-permute-done((f32[512,1]{1,0:T(8,128)S(1)}, f32[512,1]{1,0:T(8,128)S(1)}, u32[]{:S(2)}, u32[]{:S(2)}) %collective-permute-start.3) | collective-permute-done | bytes 2080 | tf_op jit(solution)/shard_map/ppermute | solution.py:38
  52.7 1.8 convolution_bitcast_fusion.3
  54.5 2.0 copy.30
  57.7 10.6 %all_to_all.62 = f32[8,1,256]{2,1,0:T(1,128)S(1)} all-to-all(f32[8,1,256]{2,1,0:T(1,128)S(1)} %broadcast_in_dim.44), channel_id=1, replica_groups=mesh['gx'=8,'gy_0'=4,'gy_1'=4,'gy_2'=2] {'gy_1','gy_2'}, dimensions={0} | all-to-all | bytes 16384 | tf_op jit(solution)/shard_map/all_to_all | solution.py:16
  68.4 15.4 %all_to_all.63 = f32[32,1,256]{2,1,0:T(1,128)S(1)} all-to-all(f32[32,1,256]{2,1,0:T(1,128)S(1)} %broadcast_in_dim.45), channel_id=1, replica_groups=mesh['gx'=8,'gy_0'=4,'gy_1'=4,'gy_2'=2] {'gx','gy_0'}, dimensions={0} | all-to-all | bytes 65536 | tf_op jit(solution)/shard_map/all_to_all | solution.py:16
  86.3 2.2 subtract_divide_fusion.2
  88.7 2.4 collective-permute-start.4
  92.4 4.5 %collective-permute-start.6 = (f32[512,1]{1,0:T(8,128)S(1)}, f32[512,1]{1,0:T(8,128)S(1)}, u32[]{:S(2)}, u32[]{:S(2)}) collective-permute-start(f32[512,1]{1,0:T(8,128)S(1)} %get-tuple-element.16), channel_id=1, source_target_pairs={{0,1},{1,2},{2,3},{3,4},{4,5},{5,6},{6,7},{7,8},{8,9},{9,10},{10,1... | collective-permute-start | bytes 6152 | tf_op jit(solution)/shard_map/ppermute | solution.py:37
  96.9 1.9 collective-permute-start.7
  98.8 1.3 collective-permute-done.6
  100.2 4.4 %collective-permute-done.7 = f32[512,1]{1,0:T(8,128)S(1)} collective-permute-done((f32[512,1]{1,0:T(8,128)S(1)}, f32[512,1]{1,0:T(8,128)S(1)}, u32[]{:S(2)}, u32[]{:S(2)}) %collective-permute-start.7) | collective-permute-done | bytes 2080 | tf_op jit(solution)/shard_map/ppermute | solution.py:38
  106.3 1.8 convolution_bitcast_fusion.2
  108.1 2.1 copy.37
  111.4 10.6 %all_to_all.64 = f32[8,1,256]{2,1,0:T(1,128)S(1)} all-to-all(f32[8,1,256]{2,1,0:T(1,128)S(1)} %broadcast_in_dim.47), channel_id=1, replica_groups=mesh['gx'=8,'gy_0'=4,'gy_1'=4,'gy_2'=2] {'gy_1','gy_2'}, dimensions={0} | all-to-all | bytes 16384 | tf_op jit(solution)/shard_map/all_to_all | solution.py:16
  122.6 6.9 %all-to-all-start.5 = ((f32[32,1,256]{2,1,0:T(1,128)}), f32[32,1,256]{2,1,0:T(1,128)S(1)}, u32[]{:S(2)}, u32[]{:S(2)}) async-start(f32[32,1,256]{2,1,0:T(1,128)} %broadcast_in_dim.48), calls=%async_computation.5 | async-start | bytes 65536 | tf_op jit(solution)/shard_map/all_to_all | solution.py:16
  130.1 8.1 %all-to-all-done.5 = f32[32,1,256]{2,1,0:T(1,128)S(1)} async-done(((f32[32,1,256]{2,1,0:T(1,128)}), f32[32,1,256]{2,1,0:T(1,128)S(1)}, u32[]{:S(2)}, u32[]{:S(2)}) %all-to-all-start.5) | async-done | bytes 32800 | tf_op jit(solution)/shard_map/all_to_all | solution.py:16
  140.6 2.9 %subtract_divide_fusion.1 = f32[512,512]{1,0:T(8,128)S(1)} fusion(f32[512,512]{1,0:T(8,128)S(1)} %subtract_divide_fusion.2, f32[512,512]{1,0:T(8,128)} %copy-done.5, f32[]{:T(128)} %sqrt.17, f32[]{:T(128)} %bitcast.20, f32[]{:T(128)} %bitcast.19, f32[512,512]{1,0:T(8,128)S(1)} %copy-done.1, f32[]{:T(128)S(6)} %sqrt.15), kind=kLoop, calls=%fused_computation.82 | loop fusion | flops 1572864 | bytes 4194320 | tf_op jit(solution)/shard_map/div | solution.py:113
  143.7 2.4 collective-permute-start.8
  146.1 1.3 collective-permute-start.9
  147.4 4.5 %collective-permute-start.10 = (f32[512,1]{1,0:T(8,128)S(1)}, f32[512,1]{1,0:T(8,128)S(1)}, u32[]{:S(2)}, u32[]{:S(2)}) collective-permute-start(f32[512,1]{1,0:T(8,128)S(1)} %get-tuple-element.12), channel_id=1, source_target_pairs={{0,1},{1,2},{2,3},{3,4},{4,5},{5,6},{6,7},{7,8},{8,9},{9,10},{10,1... | collective-permute-start | bytes 6152 | tf_op jit(solution)/shard_map/ppermute | solution.py:37
  151.9 2.1 collective-permute-start.11
  155.2 4.4 %collective-permute-done.11 = f32[512,1]{1,0:T(8,128)S(1)} collective-permute-done((f32[512,1]{1,0:T(8,128)S(1)}, f32[512,1]{1,0:T(8,128)S(1)}, u32[]{:S(2)}, u32[]{:S(2)}) %collective-permute-start.11) | collective-permute-done | bytes 2080 | tf_op jit(solution)/shard_map/ppermute | solution.py:38
  161.4 1.8 convolution_bitcast_fusion.1
  163.2 2.1 copy.42
  167.1 6.2 %all-to-all-start.6 = ((f32[8,1,256]{2,1,0:T(1,128)}), f32[8,1,256]{2,1,0:T(1,128)S(1)}, u32[]{:S(2)}, u32[]{:S(2)}) async-start(f32[8,1,256]{2,1,0:T(1,128)} %broadcast_in_dim.50), calls=%async_computation.6 | async-start | bytes 16384 | tf_op jit(solution)/shard_map/all_to_all | solution.py:16
  173.9 3.9 %all-to-all-done.6 = f32[8,1,256]{2,1,0:T(1,128)S(1)} async-done(((f32[8,1,256]{2,1,0:T(1,128)}), f32[8,1,256]{2,1,0:T(1,128)S(1)}, u32[]{:S(2)}, u32[]{:S(2)}) %all-to-all-start.6) | async-done | bytes 8224 | tf_op jit(solution)/shard_map/all_to_all | solution.py:16
  178.5 6.9 %all-to-all-start.7 = ((f32[32,1,256]{2,1,0:T(1,128)}), f32[32,1,256]{2,1,0:T(1,128)S(1)}, u32[]{:S(2)}, u32[]{:S(2)}) async-start(f32[32,1,256]{2,1,0:T(1,128)} %broadcast_in_dim.51), calls=%async_computation.7 | async-start | bytes 65536 | tf_op jit(solution)/shard_map/all_to_all | solution.py:16
  185.4 8.7 %all-to-all-done.7 = f32[32,1,256]{2,1,0:T(1,128)S(1)} async-done(((f32[32,1,256]{2,1,0:T(1,128)}), f32[32,1,256]{2,1,0:T(1,128)S(1)}, u32[]{:S(2)}, u32[]{:S(2)}) %all-to-all-start.7) | async-done | bytes 32800 | tf_op jit(solution)/shard_map/all_to_all | solution.py:16
  196.3 4.0 %subtract_divide_fusion = f32[512,512]{1,0:T(8,128)S(1)} fusion(f32[512,512]{1,0:T(8,128)} %copy-done.2, f32[512,512]{1,0:T(8,128)S(1)} %subtract_divide_fusion.2, f32[512,512]{1,0:T(8,128)} %copy-done.3, f32[]{:T(128)} %sqrt.18, f32[]{:T(128)} %bitcast.31, f32[]{:T(128)} %bitcast.30, f32[]{:T(128)} %bitcast.29, f32[512,512]{1,0:T(8,128)S(1)} %copy-done.1, ...), kind=kLoop, calls=%fused_computation.81 | loop fusion | flops 2097152 | bytes 5242900 | tf_op jit(solution)/shard_map/div | solution.py:113
  200.5 2.4 collective-permute-start.12
  204.2 4.5 %collective-permute-start.14 = (f32[512,1]{1,0:T(8,128)S(1)}, f32[512,1]{1,0:T(8,128)S(1)}, u32[]{:S(2)}, u32[]{:S(2)}) collective-permute-start(f32[512,1]{1,0:T(8,128)S(1)} %get-tuple-element.8), channel_id=1, source_target_pairs={{0,1},{1,2},{2,3},{3,4},{4,5},{5,6},{6,7},{7,8},{8,9},{9,10},{10,1... | collective-permute-start | bytes 6152 | tf_op jit(solution)/shard_map/ppermute | solution.py:37
  208.6 1.9 collective-permute-start.15
  211.9 4.4 %collective-permute-done.15 = f32[512,1]{1,0:T(8,128)S(1)} collective-permute-done((f32[512,1]{1,0:T(8,128)S(1)}, f32[512,1]{1,0:T(8,128)S(1)}, u32[]{:S(2)}, u32[]{:S(2)}) %collective-permute-start.15) | collective-permute-done | bytes 2080 | tf_op jit(solution)/shard_map/ppermute | solution.py:38
  218.1 1.8 convolution_bitcast_fusion
  220.0 2.1 copy.47
  223.8 6.3 %all-to-all-start.8 = ((f32[8,1,256]{2,1,0:T(1,128)}), f32[8,1,256]{2,1,0:T(1,128)S(1)}, u32[]{:S(2)}, u32[]{:S(2)}) async-start(f32[8,1,256]{2,1,0:T(1,128)} %broadcast_in_dim.53), calls=%async_computation.8 | async-start | bytes 16384 | tf_op jit(solution)/shard_map/all_to_all | solution.py:16
  230.1 4.6 %all-to-all-done.8 = f32[8,1,256]{2,1,0:T(1,128)S(1)} async-done(((f32[8,1,256]{2,1,0:T(1,128)}), f32[8,1,256]{2,1,0:T(1,128)S(1)}, u32[]{:S(2)}, u32[]{:S(2)}) %all-to-all-start.8) | async-done | bytes 8224 | tf_op jit(solution)/shard_map/all_to_all | solution.py:16
  235.3 6.8 %all-to-all-start.9 = ((f32[32,1,256]{2,1,0:T(1,128)}), f32[32,1,256]{2,1,0:T(1,128)S(1)}, u32[]{:S(2)}, u32[]{:S(2)}) async-start(f32[32,1,256]{2,1,0:T(1,128)} %broadcast_in_dim.54), calls=%async_computation.9 | async-start | bytes 65536 | tf_op jit(solution)/shard_map/all_to_all | solution.py:16
  242.2 8.6 %all-to-all-done.9 = f32[32,1,256]{2,1,0:T(1,128)S(1)} async-done(((f32[32,1,256]{2,1,0:T(1,128)}), f32[32,1,256]{2,1,0:T(1,128)S(1)}, u32[]{:S(2)}, u32[]{:S(2)}) %all-to-all-start.9) | async-done | bytes 32800 | tf_op jit(solution)/shard_map/all_to_all | solution.py:16
  270.8 5.2 %multiply_subtract_fusion = (f32[512,512]{1,0:T(8,128)}, f32[512,512]{1,0:T(8,128)}) fusion(f32[512,512]{1,0:T(8,128)} %copy-done.16, f32[512,512]{1,0:T(8,128)} %copy-done.3, f32[512,512]{1,0:T(8,128)} %copy-done.5, f32[512,512]{1,0:T(8,128)S(1)} %copy-done.1, f32[512,512]{1,0:T(8,128)} %copy-done.4, f32[]{:T(128)S(6)} %div.107, f32[]{:T(128)S(6)} %div.108, ...), kind=kLoop, calls=%fused_computation.79 | loop fusion | flops 4194304 | bytes 10485780 | tf_op jit(solution)/shard_map/sub | solution.py:126
  (119 shorter events, 32.7 us)
Async XLA Ops:
  0.6 1.0 copy-start
  1.7 2.5 copy-start.14
  4.0 31.7 %copy-start.1 = (f32[512,512]{1,0:T(8,128)S(1)}, f32[512,512]{1,0:T(8,128)}, u32[]{:S(2)}) copy-start(f32[512,512]{1,0:T(8,128)} %param.5) | copy-start | bytes 3145732
  35.7 16.2 %copy-start.10 = (f32[512,512]{1,0:T(8,128)S(1)}, f32[512,512]{1,0:T(8,128)}, u32[]{:S(2)}) copy-start(f32[512,512]{1,0:T(8,128)} %param.6) | copy-start | bytes 3145732
  35.8 16.0 %copy-start.6 = (f32[512,512]{1,0:T(8,128)S(1)}, f32[512,512]{1,0:T(8,128)}, u32[]{:S(2)}) copy-start(f32[512,512]{1,0:T(8,128)} %param.7) | copy-start | bytes 3145732
  36.0 10.1 %collective-permute-start = (f32[1,512]{1,0:T(1,128)S(1)}, f32[1,512]{1,0:T(1,128)S(1)}, u32[]{:S(2)}, u32[]{:S(2)}) collective-permute-start(f32[1,512]{1,0:T(1,128)S(1)} %get-tuple-element.22), channel_id=1, source_target_pairs={{0,32},{32,64},{64,96},{96,128},{128,160},{160,192},{192,224},{1,3... | collective-permute-start | bytes 6152 | tf_op jit(solution)/shard_map/ppermute | solution.py:37
  38.4 7.7 %collective-permute-start.1 = (f32[1,512]{1,0:T(1,128)S(1)}, f32[1,512]{1,0:T(1,128)S(1)}, u32[]{:S(2)}, u32[]{:S(2)}) collective-permute-start(f32[1,512]{1,0:T(1,128)S(1)} %get-tuple-element.23), channel_id=1, source_target_pairs={{32,0},{64,32},{96,64},{128,96},{160,128},{192,160},{224,192},{33,... | collective-permute-start | bytes 6152 | tf_op jit(solution)/shard_map/ppermute | solution.py:38
  39.7 7.8 %collective-permute-start.2 = (f32[512,1]{1,0:T(8,128)S(1)}, f32[512,1]{1,0:T(8,128)S(1)}, u32[]{:S(2)}, u32[]{:S(2)}) collective-permute-start(f32[512,1]{1,0:T(8,128)S(1)} %get-tuple-element.20), channel_id=1, source_target_pairs={{0,1},{1,2},{2,3},{3,4},{4,5},{5,6},{6,7},{7,8},{8,9},{9,10},{10,1... | collective-permute-start | bytes 6152 | tf_op jit(solution)/shard_map/ppermute | solution.py:37
  44.2 7.7 %collective-permute-start.3 = (f32[512,1]{1,0:T(8,128)S(1)}, f32[512,1]{1,0:T(8,128)S(1)}, u32[]{:S(2)}, u32[]{:S(2)}) collective-permute-start(f32[512,1]{1,0:T(8,128)S(1)} %get-tuple-element.21), channel_id=1, source_target_pairs={{1,0},{2,1},{3,2},{4,3},{5,4},{6,5},{7,6},{8,7},{9,8},{10,9},{11,1... | collective-permute-start | bytes 6152 | tf_op jit(solution)/shard_map/ppermute | solution.py:38
  52.7 1.8 copy-start.4
  86.3 18.2 %copy-start.11 = (f32[512,512]{1,0:T(8,128)S(1)}, f32[512,512]{1,0:T(8,128)}, u32[]{:S(2)}) copy-start(f32[512,512]{1,0:T(8,128)} %param.6) | copy-start | bytes 3145732
  88.5 16.0 %copy-start.7 = (f32[512,512]{1,0:T(8,128)S(1)}, f32[512,512]{1,0:T(8,128)}, u32[]{:S(2)}) copy-start(f32[512,512]{1,0:T(8,128)} %param.7) | copy-start | bytes 3145732
  88.7 10.1 %collective-permute-start.4 = (f32[1,512]{1,0:T(1,128)S(1)}, f32[1,512]{1,0:T(1,128)S(1)}, u32[]{:S(2)}, u32[]{:S(2)}) collective-permute-start(f32[1,512]{1,0:T(1,128)S(1)} %get-tuple-element.18), channel_id=1, source_target_pairs={{0,32},{32,64},{64,96},{96,128},{128,160},{160,192},{192,224},{1,3... | collective-permute-start | bytes 6152 | tf_op jit(solution)/shard_map/ppermute | solution.py:37
  91.1 7.7 %collective-permute-start.5 = (f32[1,512]{1,0:T(1,128)S(1)}, f32[1,512]{1,0:T(1,128)S(1)}, u32[]{:S(2)}, u32[]{:S(2)}) collective-permute-start(f32[1,512]{1,0:T(1,128)S(1)} %get-tuple-element.19), channel_id=1, source_target_pairs={{32,0},{64,32},{96,64},{128,96},{160,128},{192,160},{224,192},{33,... | collective-permute-start | bytes 6152 | tf_op jit(solution)/shard_map/ppermute | solution.py:38
  92.4 7.8 %collective-permute-start.6 = (f32[512,1]{1,0:T(8,128)S(1)}, f32[512,1]{1,0:T(8,128)S(1)}, u32[]{:S(2)}, u32[]{:S(2)}) collective-permute-start(f32[512,1]{1,0:T(8,128)S(1)} %get-tuple-element.16), channel_id=1, source_target_pairs={{0,1},{1,2},{2,3},{3,4},{4,5},{5,6},{6,7},{7,8},{8,9},{9,10},{10,1... | collective-permute-start | bytes 6152 | tf_op jit(solution)/shard_map/ppermute | solution.py:37
  96.9 7.7 %collective-permute-start.7 = (f32[512,1]{1,0:T(8,128)S(1)}, f32[512,1]{1,0:T(8,128)S(1)}, u32[]{:S(2)}, u32[]{:S(2)}) collective-permute-start(f32[512,1]{1,0:T(8,128)S(1)} %get-tuple-element.17), channel_id=1, source_target_pairs={{1,0},{2,1},{3,2},{4,3},{5,4},{6,5},{7,6},{8,7},{9,8},{10,9},{11,1... | collective-permute-start | bytes 6152 | tf_op jit(solution)/shard_map/ppermute | solution.py:38
  105.4 1.0 copy-start.5
  122.6 15.6 %all-to-all-start.5 = ((f32[32,1,256]{2,1,0:T(1,128)}), f32[32,1,256]{2,1,0:T(1,128)S(1)}, u32[]{:S(2)}, u32[]{:S(2)}) async-start(f32[32,1,256]{2,1,0:T(1,128)} %broadcast_in_dim.48), calls=%async_computation.5 | async-start | bytes 65536 | tf_op jit(solution)/shard_map/all_to_all | solution.py:16
  140.6 19.0 %copy-start.12 = (f32[512,512]{1,0:T(8,128)S(1)}, f32[512,512]{1,0:T(8,128)}, u32[]{:S(2)}) copy-start(f32[512,512]{1,0:T(8,128)} %param.6) | copy-start | bytes 3145732
  143.5 16.9 %copy-start.2 = (f32[512,512]{1,0:T(8,128)}, f32[512,512]{1,0:T(8,128)S(1)}, u32[]{:S(2)}) copy-start(f32[512,512]{1,0:T(8,128)S(1)} %subtract_divide_fusion.1) | copy-start | bytes 3145732
  143.5 16.0 %copy-start.8 = (f32[512,512]{1,0:T(8,128)S(1)}, f32[512,512]{1,0:T(8,128)}, u32[]{:S(2)}) copy-start(f32[512,512]{1,0:T(8,128)} %param.7) | copy-start | bytes 3145732
  143.7 10.3 %collective-permute-start.8 = (f32[1,512]{1,0:T(1,128)S(1)}, f32[1,512]{1,0:T(1,128)S(1)}, u32[]{:S(2)}, u32[]{:S(2)}) collective-permute-start(f32[1,512]{1,0:T(1,128)S(1)} %get-tuple-element.14), channel_id=1, source_target_pairs={{0,32},{32,64},{64,96},{96,128},{128,160},{160,192},{192,224},{1,3... | collective-permute-start | bytes 6152 | tf_op jit(solution)/shard_map/ppermute | solution.py:37
  146.1 7.9 %collective-permute-start.9 = (f32[1,512]{1,0:T(1,128)S(1)}, f32[1,512]{1,0:T(1,128)S(1)}, u32[]{:S(2)}, u32[]{:S(2)}) collective-permute-start(f32[1,512]{1,0:T(1,128)S(1)} %get-tuple-element.15), channel_id=1, source_target_pairs={{32,0},{64,32},{96,64},{128,96},{160,128},{192,160},{224,192},{33,... | collective-permute-start | bytes 6152 | tf_op jit(solution)/shard_map/ppermute | solution.py:38
  147.4 7.8 %collective-permute-start.10 = (f32[512,1]{1,0:T(8,128)S(1)}, f32[512,1]{1,0:T(8,128)S(1)}, u32[]{:S(2)}, u32[]{:S(2)}) collective-permute-start(f32[512,1]{1,0:T(8,128)S(1)} %get-tuple-element.12), channel_id=1, source_target_pairs={{0,1},{1,2},{2,3},{3,4},{4,5},{5,6},{6,7},{7,8},{8,9},{9,10},{10,1... | collective-permute-start | bytes 6152 | tf_op jit(solution)/shard_map/ppermute | solution.py:37
  151.9 7.7 %collective-permute-start.11 = (f32[512,1]{1,0:T(8,128)S(1)}, f32[512,1]{1,0:T(8,128)S(1)}, u32[]{:S(2)}, u32[]{:S(2)}) collective-permute-start(f32[512,1]{1,0:T(8,128)S(1)} %get-tuple-element.13), channel_id=1, source_target_pairs={{1,0},{2,1},{3,2},{4,3},{5,4},{6,5},{7,6},{8,7},{9,8},{10,9},{11,1... | collective-permute-start | bytes 6152 | tf_op jit(solution)/shard_map/ppermute | solution.py:38
  160.4 1.0 copy-start.3
  167.1 10.8 %all-to-all-start.6 = ((f32[8,1,256]{2,1,0:T(1,128)}), f32[8,1,256]{2,1,0:T(1,128)S(1)}, u32[]{:S(2)}, u32[]{:S(2)}) async-start(f32[8,1,256]{2,1,0:T(1,128)} %broadcast_in_dim.50), calls=%async_computation.6 | async-start | bytes 16384 | tf_op jit(solution)/shard_map/all_to_all | solution.py:16
  178.5 15.6 %all-to-all-start.7 = ((f32[32,1,256]{2,1,0:T(1,128)}), f32[32,1,256]{2,1,0:T(1,128)S(1)}, u32[]{:S(2)}, u32[]{:S(2)}) async-start(f32[32,1,256]{2,1,0:T(1,128)} %broadcast_in_dim.51), calls=%async_computation.7 | async-start | bytes 65536 | tf_op jit(solution)/shard_map/all_to_all | solution.py:16
  196.3 20.0 %copy-start.13 = (f32[512,512]{1,0:T(8,128)S(1)}, f32[512,512]{1,0:T(8,128)}, u32[]{:S(2)}) copy-start(f32[512,512]{1,0:T(8,128)} %param.6) | copy-start | bytes 3145732
  200.3 16.9 %copy-start.15 = (f32[512,512]{1,0:T(8,128)}, f32[512,512]{1,0:T(8,128)S(1)}, u32[]{:S(2)}) copy-start(f32[512,512]{1,0:T(8,128)S(1)} %subtract_divide_fusion) | copy-start | bytes 3145732
  200.3 16.0 %copy-start.9 = (f32[512,512]{1,0:T(8,128)S(1)}, f32[512,512]{1,0:T(8,128)}, u32[]{:S(2)}) copy-start(f32[512,512]{1,0:T(8,128)} %param.7) | copy-start | bytes 3145732
  200.5 10.2 %collective-permute-start.12 = (f32[1,512]{1,0:T(1,128)S(1)}, f32[1,512]{1,0:T(1,128)S(1)}, u32[]{:S(2)}, u32[]{:S(2)}) collective-permute-start(f32[1,512]{1,0:T(1,128)S(1)} %get-tuple-element.10), channel_id=1, source_target_pairs={{0,32},{32,64},{64,96},{96,128},{128,160},{160,192},{192,224},{1,3... | collective-permute-start | bytes 6152 | tf_op jit(solution)/shard_map/ppermute | solution.py:37
  202.9 7.8 %collective-permute-start.13 = (f32[1,512]{1,0:T(1,128)S(1)}, f32[1,512]{1,0:T(1,128)S(1)}, u32[]{:S(2)}, u32[]{:S(2)}) collective-permute-start(f32[1,512]{1,0:T(1,128)S(1)} %get-tuple-element.11), channel_id=1, source_target_pairs={{32,0},{64,32},{96,64},{128,96},{160,128},{192,160},{224,192},{33,... | collective-permute-start | bytes 6152 | tf_op jit(solution)/shard_map/ppermute | solution.py:38
  204.2 7.8 %collective-permute-start.14 = (f32[512,1]{1,0:T(8,128)S(1)}, f32[512,1]{1,0:T(8,128)S(1)}, u32[]{:S(2)}, u32[]{:S(2)}) collective-permute-start(f32[512,1]{1,0:T(8,128)S(1)} %get-tuple-element.8), channel_id=1, source_target_pairs={{0,1},{1,2},{2,3},{3,4},{4,5},{5,6},{6,7},{7,8},{8,9},{9,10},{10,1... | collective-permute-start | bytes 6152 | tf_op jit(solution)/shard_map/ppermute | solution.py:37
  208.6 7.7 %collective-permute-start.15 = (f32[512,1]{1,0:T(8,128)S(1)}, f32[512,1]{1,0:T(8,128)S(1)}, u32[]{:S(2)}, u32[]{:S(2)}) collective-permute-start(f32[512,1]{1,0:T(8,128)S(1)} %get-tuple-element.9), channel_id=1, source_target_pairs={{1,0},{2,1},{3,2},{4,3},{5,4},{6,5},{7,6},{8,7},{9,8},{10,9},{11,1... | collective-permute-start | bytes 6152 | tf_op jit(solution)/shard_map/ppermute | solution.py:38
  217.2 1.0 copy-start.16
  223.8 10.9 %all-to-all-start.8 = ((f32[8,1,256]{2,1,0:T(1,128)}), f32[8,1,256]{2,1,0:T(1,128)S(1)}, u32[]{:S(2)}, u32[]{:S(2)}) async-start(f32[8,1,256]{2,1,0:T(1,128)} %broadcast_in_dim.53), calls=%async_computation.8 | async-start | bytes 16384 | tf_op jit(solution)/shard_map/all_to_all | solution.py:16
  235.3 15.5 %all-to-all-start.9 = ((f32[32,1,256]{2,1,0:T(1,128)}), f32[32,1,256]{2,1,0:T(1,128)S(1)}, u32[]{:S(2)}, u32[]{:S(2)}) async-start(f32[32,1,256]{2,1,0:T(1,128)} %broadcast_in_dim.54), calls=%async_computation.9 | async-start | bytes 65536 | tf_op jit(solution)/shard_map/all_to_all | solution.py:16
where the time goes:
time: 278 us; the launch traced here: 276 us
  starting transfers between devices  73.4 us (26%)
  blocking collectives  66.5 us (24%)
  waiting for transfers between devices  56.6 us (20%)
  other arithmetic  30.3 us (11%)
  between operations  19.8 us (7%)
  local copies, waits for them, and re-layouts  18.8 us (7%)
  matrix products  10.5 us (4%)
    all_to_all x5, blocking collectives, sent_to_all(): return lax.all_to_all(copies, axis, split_axis=0, concat_axis=0, tiled=True)  66.5 us
    all_to_all x5, waiting for transfers between devices, sent_to_all(): return lax.all_to_all(copies, axis, split_axis=0, concat_axis=0, tiled=True)  33.9 us
    all_to_all x5, starting transfers between devices, sent_to_all(): return lax.all_to_all(copies, axis, split_axis=0, concat_axis=0, tiled=True)  33 us
    ppermute x8, starting transfers between devices, with_halo(): lax.ppermute(last, axis, up)  27.4 us
    ppermute x8, waiting for transfers between devices, with_halo(): lax.ppermute(initial, axis, [(b, a) for a, b in up])  17.6 us
    ppermute x8, starting transfers between devices, with_halo(): lax.ppermute(initial, axis, [(b, a) for a, b in up])  13 us
    unnamed x39, local copies, waits for them, and re-layouts  12.5 us
    dot_general x5, matrix products, sketch(): product = jnp.dot(field, sketch_cols.T, precision=lax.Precision.HIGHEST)  9.57 us
  transfers between devices with their start and end apart: 21, of which 13 were waited for; matrix products, arithmetic and copies ran while one was open for 1% of the time, Pallas kernels for 0%

commit v1 on v0

v1 whole, which is shorter than its diff:
```python
import functools

import jax
import jax.numpy as jnp
from jax import lax
from jax.experimental import pallas as pl
from jax.experimental.pallas import tpu as pltpu
from jax.sharding import Mesh
from jax.sharding import PartitionSpec as P

ITERS = 4
GY = ("x", "y", "c")
NEAR = ("z", "x")
FAR = ("y", "c")
F32 = jnp.float32
BF16 = jnp.bfloat16
DIAG = 4.0 + 0.05
LANES = 128
MIB = 1024 * 1024


def iota(shape, dim):
    return lax.broadcasted_iota(jnp.int32, shape, dim)


def vmem():
    return pl.BlockSpec(memory_space=pltpu.VMEM)


def params(limit=40):
    return pltpu.CompilerParams(vmem_limit_bytes=limit * MIB)


def rows_kernel(b0, x0, y0, b1, x1, y1, first, last):
    ones = jnp.ones((4, b0.shape[1]), F32)
    first[...] = jnp.concatenate([b0[0:4, :], x0[0:4, :], y0[0:4, :], ones], axis=0)
    last[...] = jnp.concatenate([b1[4:8, :], x1[4:8, :], y1[4:8, :], ones], axis=0)


def edge_rows(b, dx, dy):
    rows, width = b.shape
    low = pl.BlockSpec((8, width), lambda i: (0, 0))
    high = pl.BlockSpec((8, width), lambda i: (rows // 8 - 1, 0))
    out = pl.BlockSpec((16, width), lambda i: (0, 0))
    return pl.pallas_call(
        rows_kernel,
        grid=(1,),
        in_specs=[low] * 3 + [high] * 3,
        out_specs=[out] * 2,
        out_shape=[jax.ShapeDtypeStruct((16, width), F32)] * 2,
        name="edge_rows",
    )(b, dx, dy, b, dx, dy)


def columns_kernel(b0, x0, y0, b1, x1, y1, first, last):
    lane = iota(b0.shape, 1)
    one = jnp.ones(b0.shape, F32)
    packed = jnp.where(lane < 4, b0[...], pltpu.roll(x0[...], 4, 1))
    packed = jnp.where(lane < 8, packed, pltpu.roll(y0[...], 8, 1))
    packed = jnp.where(lane < 12, packed, one)
    first[...] = packed.T[0:16, :]
    packed = jnp.where(lane < 4, pltpu.roll(b1[...], 4, 1), pltpu.roll(x1[...], 8, 1))
    packed = jnp.where(lane < 8, packed, pltpu.roll(y1[...], 12, 1))
    packed = jnp.where(lane < 12, packed, one)
    last[...] = packed.T[0:16, :]


def edge_columns(b, dx, dy):
    rows, width = b.shape
    low = pl.BlockSpec((rows, LANES), lambda i: (0, 0))
    high = pl.BlockSpec((rows, LANES), lambda i: (0, width // LANES - 1))
    out = pl.BlockSpec((16, rows), lambda i: (0, 0))
    return pl.pallas_call(
        columns_kernel,
        grid=(1,),
        in_specs=[low] * 3 + [high] * 3,
        out_specs=[out] * 2,
        out_shape=[jax.ShapeDtypeStruct((16, rows), F32)] * 2,
        compiler_params=params(),
        name="edge_columns",
    )(b, dx, dy, b, dx, dy)


def split(value):
    high = value.astype(BF16)
    return high, (value - high.astype(F32)).astype(BF16)


def factors_kernel(cols, rows, right, rows_t):
    high, low = split(cols[...].T)
    n = high.shape[0]
    right[0:n, :] = high
    right[n : 2 * n, :] = high
    right[2 * n : 3 * n, :] = low
    rows_t[...] = rows[...].T


def factors(sketch_cols, sketch_rows):
    k, n = sketch_cols.shape
    m = sketch_rows.shape[1]
    return pl.pallas_call(
        factors_kernel,
        out_shape=[jax.ShapeDtypeStruct((3 * n, k), BF16), jax.ShapeDtypeStruct((m, k), F32)],
        in_specs=[vmem()] * 2,
        out_specs=[vmem()] * 2,
        compiler_params=params(),
        name="factors",
    )(sketch_cols, sketch_rows)


def neighbours(prev, cur, nxt):
    rows, width = cur.shape
    row = iota(cur.shape, 0)
    up = jnp.where(row == 0, prev[7:8, :], pltpu.roll(cur, 1, 0))
    down = jnp.where(row == rows - 1, nxt[0:1, :], pltpu.roll(cur, rows - 1, 0))
    left = pltpu.roll(cur, 1, 1)
    right = pltpu.roll(cur, width - 1, 1)
    return up, down, left, right


def krylov_kernel(
    copies, b, dx, dy, right, rows_t, top, bottom, from_left, from_right,
    t0, t1, t2, t3, t4, out, split_ref, side_dx, side_dy, side_one, tb_dx, tb_dy, tb_one, turn,
):
    rows, width = b.shape
    full = width + LANES
    lane = iota((rows, LANES), 1)
    inside = (lane < 4) | (lane >= LANES - 4)
    turn[...] = jnp.zeros_like(turn)
    for group in range(4):
        turn[8 * group : 8 * group + 4, :] = from_right[4 * group : 4 * group + 4, 0:rows]
        at = (8 * group - 4) % LANES
        turn[at : at + 4, :] = from_left[4 * group : 4 * group + 4, 0:rows]
    turned = turn[...].T
    zero = jnp.zeros((rows, LANES), F32)
    t0[0:rows + 16, width:full] = jnp.zeros((rows + 16, LANES), F32)
    t0[8 : rows + 8, width:full] = jnp.where(inside, turned, zero)
    side_dx[...] = jnp.where(inside, pltpu.roll(turned, LANES - 8, 1), zero)
    side_dy[...] = jnp.where(inside, pltpu.roll(turned, LANES - 16, 1), zero)
    side_one[...] = jnp.where(inside, pltpu.roll(turned, LANES - 24, 1), zero)
    t0[8 : rows + 8, 0:width] = b[...]
    lane = iota((4, LANES), 1)
    zero = jnp.zeros((4, LANES), F32)
    blank = jnp.zeros((4, full), F32)

    def strip(main, at, group):
        part = slice(4 * group, 4 * group + 4)
        corner = jnp.where(lane < 4, from_right[part, at : at + LANES], zero)
        corner = jnp.where(lane >= LANES - 4, from_left[part, at : at + LANES], corner)
        return jnp.concatenate([main[part, :], corner], axis=1)

    def above(group):
        return jnp.concatenate([blank, strip(top, rows, group)], axis=0)

    def below(group):
        return jnp.concatenate([strip(bottom, rows + LANES, group), blank], axis=0)

    t0[0:8, :] = above(0)
    t0[rows + 8 : rows + 16, :] = below(0)
    for ref, group in ((tb_dx, 1), (tb_dy, 2), (tb_one, 3)):
        ref[0:8, :] = above(group)
        ref[8:16, :] = below(group)

    fields = (t0, t1, t2, t3, t4)

    def advance(k, at, count, drift_x, drift_y, one):
        old = fields[k]
        cur = old[pl.ds(at, count), :]
        prev = old[pl.ds(max(at - 8, 0) if isinstance(at, int) else pl.multiple_of(at - 8, 8), 8), :]
        after = min(at + count, rows + 8) if isinstance(at, int) else pl.multiple_of(at + count, 8)
        nxt = old[pl.ds(after, 8), :]
        up, down, left, right_ = neighbours(prev, cur, nxt)
        cross = up + down + (left + right_)
        if one is not None:
            cross = jnp.concatenate([cross[:, :width], cross[:, width:] * one], axis=1) if one.shape[1] == LANES else cross * one
        new = cross + drift_x * (up - down) + drift_y * (left - right_)
        if k == 0:
            return 0.25 * new
        return 0.5 * new - fields[k - 1][pl.ds(at, count), :]

    def keep(at, value):
        high, low = split(value)
        split_ref[pl.ds(at, 16), 0:width] = high
        split_ref[pl.ds(at, 16), width : 2 * width] = low
        split_ref[pl.ds(at, 16), 2 * width : 3 * width] = high

    total = []

    def sketch():
        product = jnp.dot(split_ref[...], right[...], preferred_element_type=F32)
        total.append(jnp.sum(product * rows_t[...], axis=0, keepdims=True))

    def first(i, carry):
        at = pl.multiple_of(i * 16, 16)
        keep(at, b[pl.ds(at, 16), :])
        return carry

    lax.fori_loop(0, rows // 16, first, 0)
    sketch()
    for k in range(ITERS):
        new = fields[k + 1]
        if k < ITERS - 1:
            for at in (0, rows + 8):
                tb = slice(0, 8) if at == 0 else slice(8, 16)
                new[at : at + 8, :] = advance(k, at, 8, tb_dx[tb, :], tb_dy[tb, :], tb_one[tb, :])

        def block(i, carry, k=k, new=new):
            at = pl.multiple_of(i * 16, 16)
            here = pl.ds(at, 16)
            drift_x = jnp.concatenate([dx[here, :], side_dx[here, :]], axis=1)
            drift_y = jnp.concatenate([dy[here, :], side_dy[here, :]], axis=1)
            value = advance(k, pl.multiple_of(at + 8, 8), 16, drift_x, drift_y, side_one[here, :])
            if k < ITERS - 1:
                new[pl.ds(pl.multiple_of(at + 8, 8), 16), :] = value
            else:
                new[here, :] = value[:, :width]
            keep(at, value[:, :width])
            return carry

        lax.fori_loop(0, rows // 16, block, 0, unroll=2)
        sketch()
    whole = jnp.concatenate(total, axis=1)
    for i in range(copies):
        out[i] = whole


def krylov(b, dx, dy, right, rows_t, top, bottom, from_left, from_right, copies):
    rows, width = b.shape
    full = width + LANES
    k = rows_t.shape[1]
    padded = jax.ShapeDtypeStruct((rows + 16, full), F32)
    return pl.pallas_call(
        functools.partial(krylov_kernel, copies),
        out_shape=[padded] * 4
        + [jax.ShapeDtypeStruct((rows, width), F32), jax.ShapeDtypeStruct((copies, 1, (ITERS + 1) * k), F32)],
        in_specs=[vmem()] * 9,
        out_specs=[vmem()] * 6,
        scratch_shapes=[
            pltpu.VMEM((rows, 3 * width), BF16),
            pltpu.VMEM((rows, LANES), F32),
            pltpu.VMEM((rows, LANES), F32),
            pltpu.VMEM((rows, LANES), F32),
            pltpu.VMEM((16, full), F32),
            pltpu.VMEM((16, full), F32),
            pltpu.VMEM((16, full), F32),
            pltpu.VMEM((LANES, rows), F32),
        ],
        compiler_params=params(),
        name="krylov",
    )(b, dx, dy, right, rows_t, top, bottom, from_left, from_right)


def combine_kernel(parts, t0, t1, t2, t3, t4, sol, res, coef):
    @pl.when(pl.program_id(0) == 0)
    def _():
        k = parts.shape[2] // (ITERS + 1)
        whole = parts[0]
        for i in range(1, parts.shape[0]):
            whole = whole + parts[i]
        s = [whole[:, i * k : (i + 1) * k] for i in range(ITERS + 1)]
        images = [DIAG * s[0] - 4.0 * s[1]]
        for i in range(1, ITERS):
            images.append(DIAG * s[i] - 2.0 * (s[i + 1] + s[i - 1]))
        left = jnp.concatenate(images + [s[0]] + [jnp.zeros_like(s[0])] * (7 - ITERS), axis=0)
        ratios = []
        row = iota((8, 1), 0)
        for j in range(ITERS):
            q = left[j : j + 1, :]
            dots = jnp.sum(left * q, axis=1, keepdims=True)
            ratio = dots / dots[j : j + 1, :]
            ratios.append(ratio)
            left = left - jnp.where(row > j, ratio, 0.0) * q
        c = [None] * ITERS
        for j in reversed(range(ITERS)):
            value = ratios[j][ITERS : ITERS + 1, :]
            for i in range(j + 1, ITERS):
                value = value - ratios[j][i : i + 1, :] * c[i]
            c[j] = value
        d = [
            1.0 - DIAG * c[0] + 2.0 * c[1],
            4.0 * c[0] - DIAG * c[1] + 2.0 * c[2],
            2.0 * c[1] - DIAG * c[2] + 2.0 * c[3],
            2.0 * c[2] - DIAG * c[3],
            2.0 * c[3],
        ]
        for i, value in enumerate(c + d):
            coef[i] = jnp.broadcast_to(value, coef.shape[1:])

    rows, width = sol.shape

    def block(i, carry):
        at = pl.multiple_of(i * 8, 8)
        start = pl.multiple_of(pl.program_id(0) * rows + at, 8)
        shifted = pl.ds(pl.multiple_of(start + 8, 8), 8)
        for j in range(width // LANES):
            lanes = slice(j * LANES, (j + 1) * LANES)
            t = [ref[shifted, lanes] for ref in (t0, t1, t2, t3)] + [t4[pl.ds(start, 8), lanes]]
            first = coef[0] * t[0] + coef[1] * t[1]
            second = coef[4] * t[0] + coef[5] * t[1]
            sol[pl.ds(at, 8), lanes] = first + (coef[2] * t[2] + coef[3] * t[3])
            res[pl.ds(at, 8), lanes] = second + (coef[6] * t[2] + coef[7] * t[3]) + coef[8] * t[4]
        return carry

    lax.fori_loop(0, rows // 8, block, 0, unroll=2)


def combine(parts, fields):
    rows, width = fields[-1].shape
    steps = 4
    out = pl.BlockSpec((rows // steps, width), lambda i: (i, 0))
    return pl.pallas_call(
        combine_kernel,
        grid=(steps,),
        in_specs=[vmem()] * 6,
        out_specs=[out] * 2,
        out_shape=[jax.ShapeDtypeStruct((rows, width), F32)] * 2,
        scratch_shapes=[pltpu.VMEM((2 * ITERS + 1, 8, LANES), F32)],
        compiler_params=params(),
        name="combine",
    )(parts, *fields)


def shift(value, axis, step):
    size = lax.axis_size(axis)
    pairs = [(i, i + step) for i in range(size) if 0 <= i + step < size]
    return lax.ppermute(value, axis, pairs)


def to_all(copies, axis):
    return lax.all_to_all(copies, axis, split_axis=0, concat_axis=0, tiled=True)


def body(right_side, drift_x, drift_y, sketch_rows, sketch_cols):
    first, last = edge_rows(right_side, drift_x, drift_y)
    top, bottom = shift(last, "z", 1), shift(first, "z", -1)
    first_columns, last_columns = edge_columns(right_side, drift_x, drift_y)
    right, rows_t = factors(sketch_cols, sketch_rows)
    to_left = jnp.concatenate([first_columns, top[:, :LANES], bottom[:, :LANES]], axis=1)
    to_right = jnp.concatenate([last_columns, top[:, -LANES:], bottom[:, -LANES:]], axis=1)
    from_left, from_right = shift(to_right, GY, 1), shift(to_left, GY, -1)
    near, far = lax.axis_size(NEAR), lax.axis_size(FAR)
    *fields, partial = krylov(
        right_side, drift_x, drift_y, right, rows_t, top, bottom, from_left, from_right, near
    )
    summed = jnp.sum(to_all(partial, NEAR), axis=0, keepdims=True)
    parts = to_all(jnp.broadcast_to(summed, (far, *summed.shape[1:])), FAR)
    return tuple(combine(parts, fields))


def solution(mesh):
    split_mesh = Mesh(mesh.devices.reshape(mesh.shape["gx"], 4, 4, 2), ("z", *GY))
    in_specs = (P("z", GY), P("z", GY), P("z", GY), P(None, "z"), P(None, GY))
    out_specs = (P("z", GY), P("z", GY))
    return jax.shard_map(body, mesh=split_mesh, in_specs=in_specs, out_specs=out_specs, check_vma=False)
```

time: 278 us -> 81.3 us (0.29)
  starting transfers between devices: 73.4 us -> 12.7 us
  waiting for transfers between devices: 56.6 us -> 3.98 us
  blocking collectives: 66.5 us -> 33.1 us
  other arithmetic: 30.3 us -> 0.12 us
  between operations: 19.8 us -> 0.81 us
  Pallas kernels: 0 us -> 18.2 us
  matrix products: 10.5 us -> 0 us
  local copies, waits for them, and re-layouts: 18.8 us -> 11.9 us
    all_to_all x5 -> x0, waiting for transfers between devices: 33.9 us -> none  [sent_to_all(): return lax.all_to_all(copies, axis, split_axis=0, concat_axis=0, tiled=True)]
    all_to_all x5 -> x2, blocking collectives: 66.5 us -> 33.1 us  [to_all(): return lax.all_to_all(copies, axis, split_axis=0, concat_axis=0, tiled=True)]
    all_to_all x5 -> x0, starting transfers between devices: 33 us -> none  [sent_to_all(): return lax.all_to_all(copies, axis, split_axis=0, concat_axis=0, tiled=True)]
    ppermute x16 -> x4, starting transfers between devices: 40.5 us -> 12.7 us  [shift(): return lax.ppermute(value, axis, pairs)]
    ppermute x16 -> x4, waiting for transfers between devices: 22.7 us -> 3.98 us  [shift(): return lax.ppermute(value, axis, pairs)]
    pallas_call x0 -> x5, Pallas kernels: none -> 18.2 us  [the longest x1 13.2 us: krylov(): pl.pallas_call(functools.partial(krylov_kernel, copies), out_shape=[padde...]
    dot_general x12 -> x0, matrix products: 10.5 us -> none  [the longest x5 9.57 us: sketch(): product = jnp.dot(field, sketch_cols.T, precision=lax.Precision.HIGHEST)]
    div x8 -> x0, other arithmetic: 9.83 us -> none  [the longest x3 9.08 us: body(): basis_vectors.append(remainder / new_norm)]
  transfers between devices with their start and end apart: 21 -> 4, of which waited for: 13 -> 2; matrix products, arithmetic and copies ran while one was open for 1% -> 0% of each run, Pallas kernels for 0% -> 1%
where the time goes in v1:
time: 81.3 us; the launch traced here: 80.9 us
  blocking collectives  33.1 us (41%)
  Pallas kernels  18.2 us (22%)
  starting transfers between devices  12.7 us (16%)
  local copies, waits for them, and re-layouts  11.9 us (15%)
  waiting for transfers between devices  3.98 us (5%)
    all_to_all x2, blocking collectives, to_all(): return lax.all_to_all(copies, axis, split_axis=0, concat_axis=0, tiled=True)  33.1 us
    pallas_call x1, Pallas kernels, krylov(): pl.pallas_call(functools.partial(krylov_kernel, copies), out_shape=[padde...  13.2 us
    ppermute x4, starting transfers between devices, shift(): return lax.ppermute(value, axis, pairs)  12.7 us
    unnamed x30, local copies, waits for them, and re-layouts  11.9 us
    ppermute x4, waiting for transfers between devices, shift(): return lax.ppermute(value, axis, pairs)  3.98 us
    pallas_call x1, Pallas kernels, combine(): pl.pallas_call(combine_kernel, grid=(steps,), in_specs=[vmem()] * 6, out_...  2.62 us
  transfers between devices with their start and end apart: 4, of which 2 were waited for; matrix products, arithmetic and copies ran while one was open for 0% of the time, Pallas kernels for 1%

profile of v1, /device:TPU:1, one launch (start us, length us, event | category | flops | bytes accessed | tf_op | source)
XLA Modules:
  0.0 80.9 jit_solution(7813240070304774528)
XLA Ops:
  0.6 0.0 copy-start.2
  0.6 0.0 copy-start.1
  0.6 0.0 copy-start
  0.7 1.6 %edge_rows.1 = (f32[16,512]{1,0:T(8,128)}, f32[16,512]{1,0:T(8,128)}) custom-call(f32[512,512]{1,0:T(8,128)} %b.1, f32[512,512]{1,0:T(8,128)} %dx.1, f32[512,512]{1,0:T(8,128)} %dy.1, f32[512,512]{1,0:T(8,128)} %b.1, f32[512,512]{1,0:T(8,128)} %dx.1, f32[512,512]{1,0:T(8,128)} %dy.1), custom_call_target="tpu_custom_call" | custom-call | tf_op jit(solution)/shard_map/edge_rows/pallas_call | solution.py:45
  2.2 4.3 %collective-permute-start = (f32[16,512]{1,0:T(8,128)}, f32[16,512]{1,0:T(8,128)S(1)}, u32[]{:S(2)}, u32[]{:S(2)}) collective-permute-start(f32[16,512]{1,0:T(8,128)} %get-tuple-element.16), channel_id=1, source_target_pairs={{0,32},{32,64},{64,96},{96,128},{128,160},{160,192},{192,224},{1,3... | collective-permute-start | bytes 98312 | tf_op jit(solution)/shard_map/ppermute | solution.py:326
  6.6 0.0 copy-start.13
  6.6 0.0 copy-start.14
  6.6 1.4 %collective-permute-start.1 = (f32[16,512]{1,0:T(8,128)}, f32[16,512]{1,0:T(8,128)S(1)}, u32[]{:S(2)}, u32[]{:S(2)}) collective-permute-start(f32[16,512]{1,0:T(8,128)} %get-tuple-element.17), channel_id=1, source_target_pairs={{32,0},{64,32},{96,64},{128,96},{160,128},{192,160},{224,192},{33,... | collective-permute-start | bytes 98312 | tf_op jit(solution)/shard_map/ppermute | solution.py:326
  8.1 0.0 copy-done.2
  8.1 0.0 copy-done.1
  8.1 0.0 copy-done
  8.1 0.5 edge_columns.1
  8.6 0.0 collective-permute-done.top
  8.6 3.2 %collective-permute-done.1.bottom = f32[16,512]{1,0:T(8,128)S(1)} collective-permute-done((f32[16,512]{1,0:T(8,128)}, f32[16,512]{1,0:T(8,128)S(1)}, u32[]{:S(2)}, u32[]{:S(2)}) %collective-permute-start.1) | collective-permute-done | bytes 32800 | tf_op jit(solution)/shard_map/ppermute | solution.py:326
  11.8 3.8 %collective-permute-start.3 = (f32[16,768]{1,0:T(8,128)S(1)}, f32[16,768]{1,0:T(8,128)S(1)}, u32[]{:S(2)}, u32[]{:S(2)}) collective-permute-start(f32[16,768]{1,0:T(8,128)S(1)} %pad_maximum_fusion.1), channel_id=1, source_target_pairs={{1,0},{2,1},{3,2},{4,3},{5,4},{6,5},{7,6},{8,7},{9,8},{10,9},{11,1... | collective-permute-start | bytes 147464 | tf_op jit(solution)/shard_map/ppermute | solution.py:326
  15.7 3.1 %collective-permute-start.2 = (f32[16,768]{1,0:T(8,128)S(1)}, f32[16,768]{1,0:T(8,128)S(1)}, u32[]{:S(2)}, u32[]{:S(2)}) collective-permute-start(f32[16,768]{1,0:T(8,128)S(1)} %pad_maximum_fusion), channel_id=1, source_target_pairs={{0,1},{1,2},{2,3},{3,4},{4,5},{5,6},{6,7},{7,8},{8,9},{9,10},{10,1... | collective-permute-start | bytes 147464 | tf_op jit(solution)/shard_map/ppermute | solution.py:326
  18.8 0.0 copy-done.13
  18.8 0.0 copy-done.14
  18.8 0.3 factors.1
  19.1 0.0 collective-permute-done.3.from_right
  19.1 0.8 collective-permute-done.2.from_left
  19.9 13.2 %krylov.1 = (f32[528,640]{1,0:T(8,128)S(1)}, f32[528,640]{1,0:T(8,128)S(1)}, f32[528,640]{1,0:T(8,128)S(1)}, f32[528,640]{1,0:T(8,128)S(1)}, f32[512,512]{1,0:T(8,128)S(1)}, /*index=5*/f32[32,1,1280]{2,1,0:T(1,128)S(1)}) custom-call(f32[512,512]{1,0:T(8,128)S(1)} %copy-done, f32[512,512]{1,0:T(8,128)S(1)} %copy-done.1, f32[512,512]{1,0:T(8,128)S(1)} %copy-done.2, ...), custom_call_target="tpu_custom_call" | custom-call | tf_op jit(solution)/shard_map/krylov/pallas_call | solution.py:232
  33.1 0.0 copy-start.3
  33.1 1.1 %copy-done.3 = f32[528,640]{1,0:T(8,128)} copy-done((f32[528,640]{1,0:T(8,128)}, f32[528,640]{1,0:T(8,128)S(1)}, u32[]{:S(2)}) %copy-start.3) | copy-done | bytes 1351704
  34.2 0.0 copy-start.5
  34.2 1.1 %copy-done.5 = f32[528,640]{1,0:T(8,128)} copy-done((f32[528,640]{1,0:T(8,128)}, f32[528,640]{1,0:T(8,128)S(1)}, u32[]{:S(2)}) %copy-start.5) | copy-done | bytes 1351704
  35.3 0.0 copy-start.7
  35.3 1.1 %copy-done.7 = f32[528,640]{1,0:T(8,128)} copy-done((f32[528,640]{1,0:T(8,128)}, f32[528,640]{1,0:T(8,128)S(1)}, u32[]{:S(2)}) %copy-start.7) | copy-done | bytes 1351704
  36.4 0.0 copy-start.9
  36.4 1.1 %copy-done.9 = f32[528,640]{1,0:T(8,128)} copy-done((f32[528,640]{1,0:T(8,128)}, f32[528,640]{1,0:T(8,128)S(1)}, u32[]{:S(2)}) %copy-start.9) | copy-done | bytes 1351704
  37.5 0.0 copy-start.11
  37.5 1.0 %copy-done.11 = f32[512,512]{1,0:T(8,128)} copy-done((f32[512,512]{1,0:T(8,128)}, f32[512,512]{1,0:T(8,128)S(1)}, u32[]{:S(2)}) %copy-start.11) | copy-done | bytes 1048600
  38.4 20.3 %all_to_all.10 = f32[32,1,1280]{2,1,0:T(1,128)S(1)} all-to-all(f32[32,1,1280]{2,1,0:T(1,128)S(1)} %get-tuple-element.20), channel_id=1, replica_groups=mesh['z'=8,'x'=4,'y'=4,'c'=2] {'z','x'}, dimensions={0} | all-to-all | bytes 327680 | tf_op jit(solution)/shard_map/all_to_all | solution.py:330
  58.7 0.1 reduce_sum.9
  58.9 12.8 %all_to_all.11.parts = f32[8,1,1280]{2,1,0:T(1,128)S(1)} all-to-all(f32[8,1,1280]{2,1,0:T(1,128)S(1)} %broadcast_in_dim.2), channel_id=1, replica_groups=mesh['z'=8,'x'=4,'y'=4,'c'=2] {'y','c'}, dimensions={0} | all-to-all | bytes 81920 | tf_op jit(solution)/shard_map/all_to_all | solution.py:330
  71.7 0.0 copy-start.4
  71.7 1.3 %copy-done.4 = f32[528,640]{1,0:T(8,128)S(1)} copy-done((f32[528,640]{1,0:T(8,128)S(1)}, f32[528,640]{1,0:T(8,128)}, u32[]{:S(2)}) %copy-start.4) | copy-done | bytes 1351704
  73.0 0.0 copy-start.6
  73.0 1.3 %copy-done.6 = f32[528,640]{1,0:T(8,128)S(1)} copy-done((f32[528,640]{1,0:T(8,128)S(1)}, f32[528,640]{1,0:T(8,128)}, u32[]{:S(2)}) %copy-start.6) | copy-done | bytes 1351704
  74.4 0.0 copy-start.8
  74.4 1.3 %copy-done.8 = f32[528,640]{1,0:T(8,128)S(1)} copy-done((f32[528,640]{1,0:T(8,128)S(1)}, f32[528,640]{1,0:T(8,128)}, u32[]{:S(2)}) %copy-start.8) | copy-done | bytes 1351704
  75.7 0.0 copy-start.10
  75.7 1.3 %copy-done.10 = f32[528,640]{1,0:T(8,128)S(1)} copy-done((f32[528,640]{1,0:T(8,128)S(1)}, f32[528,640]{1,0:T(8,128)}, u32[]{:S(2)}) %copy-start.10) | copy-done | bytes 1351704
  77.0 0.0 copy-start.12
  77.0 1.2 %copy-done.12 = f32[512,512]{1,0:T(8,128)S(1)} copy-done((f32[512,512]{1,0:T(8,128)S(1)}, f32[512,512]{1,0:T(8,128)}, u32[]{:S(2)}) %copy-start.12) | copy-done | bytes 1048600
  78.2 2.6 %combine.1 = (f32[512,512]{1,0:T(8,128)}, f32[512,512]{1,0:T(8,128)}) custom-call(f32[8,1,1280]{2,1,0:T(1,128)S(1)} %all_to_all.11.parts, f32[528,640]{1,0:T(8,128)S(1)} %copy-done.4, f32[528,640]{1,0:T(8,128)S(1)} %copy-done.6, f32[528,640]{1,0:T(8,128)S(1)} %copy-done.8, f32[528,640]{1,0:T(8,128)S(1)} %copy-done.10, f32[512,512]{1,0:T(8,128)S(1)} %copy-done.12), custom_call_target="tpu_custom_call" | custom-call | tf_op jit(solution)/shard_map/combine/pallas_call | solution.py:311
  (5 shorter events, 0.0 us)
Async XLA Ops:
  0.6 7.4 %copy-start.2 = (f32[512,512]{1,0:T(8,128)S(1)}, f32[512,512]{1,0:T(8,128)}, u32[]{:S(2)}) copy-start(f32[512,512]{1,0:T(8,128)} %dy.1) | copy-start | bytes 3145732
  0.6 7.4 %copy-start.1 = (f32[512,512]{1,0:T(8,128)S(1)}, f32[512,512]{1,0:T(8,128)}, u32[]{:S(2)}) copy-start(f32[512,512]{1,0:T(8,128)} %dx.1) | copy-start | bytes 3145732
  0.6 7.4 %copy-start = (f32[512,512]{1,0:T(8,128)S(1)}, f32[512,512]{1,0:T(8,128)}, u32[]{:S(2)}) copy-start(f32[512,512]{1,0:T(8,128)} %b.1) | copy-start | bytes 3145732
  2.2 6.4 %collective-permute-start = (f32[16,512]{1,0:T(8,128)}, f32[16,512]{1,0:T(8,128)S(1)}, u32[]{:S(2)}, u32[]{:S(2)}) collective-permute-start(f32[16,512]{1,0:T(8,128)} %get-tuple-element.16), channel_id=1, source_target_pairs={{0,32},{32,64},{64,96},{96,128},{128,160},{160,192},{192,224},{1,3... | collective-permute-start | bytes 98312 | tf_op jit(solution)/shard_map/ppermute | solution.py:326
  6.6 12.2 %copy-start.13 = (f32[256,512]{1,0:T(8,128)S(1)}, f32[256,512]{1,0:T(8,128)}, u32[]{:S(2)}) copy-start(f32[256,512]{1,0:T(8,128)} %cols.1) | copy-start | bytes 1572868
  6.6 12.2 %copy-start.14 = (f32[256,512]{1,0:T(8,128)S(1)}, f32[256,512]{1,0:T(8,128)}, u32[]{:S(2)}) copy-start(f32[256,512]{1,0:T(8,128)} %rows.1) | copy-start | bytes 1572868
  6.6 5.2 %collective-permute-start.1 = (f32[16,512]{1,0:T(8,128)}, f32[16,512]{1,0:T(8,128)S(1)}, u32[]{:S(2)}, u32[]{:S(2)}) collective-permute-start(f32[16,512]{1,0:T(8,128)} %get-tuple-element.17), channel_id=1, source_target_pairs={{32,0},{64,32},{96,64},{128,96},{160,128},{192,160},{224,192},{33,... | collective-permute-start | bytes 98312 | tf_op jit(solution)/shard_map/ppermute | solution.py:326
  11.8 7.3 %collective-permute-start.3 = (f32[16,768]{1,0:T(8,128)S(1)}, f32[16,768]{1,0:T(8,128)S(1)}, u32[]{:S(2)}, u32[]{:S(2)}) collective-permute-start(f32[16,768]{1,0:T(8,128)S(1)} %pad_maximum_fusion.1), channel_id=1, source_target_pairs={{1,0},{2,1},{3,2},{4,3},{5,4},{6,5},{7,6},{8,7},{9,8},{10,9},{11,1... | collective-permute-start | bytes 147464 | tf_op jit(solution)/shard_map/ppermute | solution.py:326
  15.7 4.3 %collective-permute-start.2 = (f32[16,768]{1,0:T(8,128)S(1)}, f32[16,768]{1,0:T(8,128)S(1)}, u32[]{:S(2)}, u32[]{:S(2)}) collective-permute-start(f32[16,768]{1,0:T(8,128)S(1)} %pad_maximum_fusion), channel_id=1, source_target_pairs={{0,1},{1,2},{2,3},{3,4},{4,5},{5,6},{6,7},{7,8},{8,9},{9,10},{10,1... | collective-permute-start | bytes 147464 | tf_op jit(solution)/shard_map/ppermute | solution.py:326
  33.1 1.1 %copy-start.3 = (f32[528,640]{1,0:T(8,128)}, f32[528,640]{1,0:T(8,128)S(1)}, u32[]{:S(2)}) copy-start(f32[528,640]{1,0:T(8,128)S(1)} %get-tuple-element.21.t0) | copy-start | bytes 4055044
  34.2 1.1 %copy-start.5 = (f32[528,640]{1,0:T(8,128)}, f32[528,640]{1,0:T(8,128)S(1)}, u32[]{:S(2)}) copy-start(f32[528,640]{1,0:T(8,128)S(1)} %get-tuple-element.22.t1) | copy-start | bytes 4055044
  35.3 1.1 %copy-start.7 = (f32[528,640]{1,0:T(8,128)}, f32[528,640]{1,0:T(8,128)S(1)}, u32[]{:S(2)}) copy-start(f32[528,640]{1,0:T(8,128)S(1)} %get-tuple-element.23.t2) | copy-start | bytes 4055044
  36.4 1.1 %copy-start.9 = (f32[528,640]{1,0:T(8,128)}, f32[528,640]{1,0:T(8,128)S(1)}, u32[]{:S(2)}) copy-start(f32[528,640]{1,0:T(8,128)S(1)} %get-tuple-element.24.t3) | copy-start | bytes 4055044
  37.5 1.0 %copy-start.11 = (f32[512,512]{1,0:T(8,128)}, f32[512,512]{1,0:T(8,128)S(1)}, u32[]{:S(2)}) copy-start(f32[512,512]{1,0:T(8,128)S(1)} %get-tuple-element.25.t4) | copy-start | bytes 3145732
  71.7 1.3 %copy-start.4 = (f32[528,640]{1,0:T(8,128)S(1)}, f32[528,640]{1,0:T(8,128)}, u32[]{:S(2)}) copy-start(f32[528,640]{1,0:T(8,128)} %copy-done.3) | copy-start | bytes 4055044
  73.0 1.3 %copy-start.6 = (f32[528,640]{1,0:T(8,128)S(1)}, f32[528,640]{1,0:T(8,128)}, u32[]{:S(2)}) copy-start(f32[528,640]{1,0:T(8,128)} %copy-done.5) | copy-start | bytes 4055044
  74.4 1.3 %copy-start.8 = (f32[528,640]{1,0:T(8,128)S(1)}, f32[528,640]{1,0:T(8,128)}, u32[]{:S(2)}) copy-start(f32[528,640]{1,0:T(8,128)} %copy-done.7) | copy-start | bytes 4055044
  75.7 1.3 %copy-start.10 = (f32[528,640]{1,0:T(8,128)S(1)}, f32[528,640]{1,0:T(8,128)}, u32[]{:S(2)}) copy-start(f32[528,640]{1,0:T(8,128)} %copy-done.9) | copy-start | bytes 4055044
  77.0 1.2 %copy-start.12 = (f32[512,512]{1,0:T(8,128)S(1)}, f32[512,512]{1,0:T(8,128)}, u32[]{:S(2)}) copy-start(f32[512,512]{1,0:T(8,128)} %copy-done.11) | copy-start | bytes 3145732
